TPU v7x, 32 devices: a whole 2x2x4 slice. The times are simulated.
32 devices in a mesh: seq: 4 (over z), uly: 4 (over y, x), rep: 2 (over core).
Axes of the slice: x: 2, y: 2, z: 4, core: 2. Of those that a mesh axis runs over, the one named last changes fastest.
Arguments:
- queries: bfloat16 [4096, 2048], P(('rep', 'seq', 'uly')), parts along dimension 0, may hold values from -6 to 6
- keys: bfloat16 [4096, 2048], P(('rep', 'seq', 'uly')), parts along dimension 0, may hold values from -6 to 6
- values: bfloat16 [4096, 2048], P(('rep', 'seq', 'uly')), parts along dimension 0, may hold values from -6 to 6
- past_outputs: bfloat16 [2, 4096, 2048], P(None, ('rep', 'seq', 'uly')), parts along dimension 1, may hold values from -6 to 6
- dwa_slot: int32 [2], replicated, may hold values from 0 to 63
- dwa_table: float32 [2, 64], replicated, may hold values from 0.1 to 0.6
Outputs:
- mixed: bfloat16 [4096, 2048], P(('rep', 'seq', 'uly')), parts along dimension 0
There are 2 independent parts, one for each index of `rep`. A program takes and returns all parts, laid end to end along the dimension named above; an argument that names none is the same for every part. Nothing has to cross between parts.
All inputs are finite; a program needn't handle non-finite values.
Results may differ from a plain program's by a relative error of at most 0.0034.
Values may be sent and summed in bfloat16 or wider, within the bound.
No kernel may reach another device: no remote copies, remote signals or barrier semaphores. Data moves between devices by JAX's collectives and lax.ppermute only.
A program may use at most 64 MiB of HBM per device.

v0:
```python
import jax
import jax.numpy as jnp
from jax import lax
from jax.sharding import PartitionSpec as P

HEAD_DIM = 128


def from_behind(block, axis, distance):
    devices = range(lax.axis_size(axis))
    route = [(i - distance, i) for i in devices if i - distance in devices]
    return lax.ppermute(block, axis, route)


def block_update(state, query_heads, key_heads, value_heads, allowed):
    running, total, accumulated = state
    scores = jnp.einsum("qhd,khd->hqk", query_heads, key_heads, preferred_element_type=jnp.float32)
    scores = scores * (1.0 / HEAD_DIM**0.5)
    scores = jnp.where(allowed, scores, -jnp.inf)
    new_max = jnp.maximum(running, jnp.max(scores, axis=2))
    factor = jnp.exp(running - new_max)
    prob = jnp.exp(scores - new_max[:, :, None])
    total = total * factor + jnp.sum(prob, axis=2)
    weights = prob.astype(jnp.bfloat16)
    update = jnp.einsum("hqk,khd->qhd", weights, value_heads, preferred_element_type=jnp.float32)
    accumulated = accumulated * jnp.transpose(factor)[:, :, None] + update
    return (new_max, total, accumulated)


def shards(queries, keys, values, past_outputs, dwa_slot, dwa_table):
    n_uly = lax.axis_size("uly")
    n_seq = lax.axis_size("seq")
    span_size = min(4, n_seq)
    features = queries.shape[1]
    local_heads = features // n_uly // HEAD_DIM
    query_rows, key_rows, value_rows = (
        lax.all_to_all(queries, "uly", split_axis=1, concat_axis=0, tiled=True),
        lax.all_to_all(keys, "uly", split_axis=1, concat_axis=0, tiled=True),
        lax.all_to_all(values, "uly", split_axis=1, concat_axis=0, tiled=True),
    )
    row_count = query_rows.shape[0]
    split_shape = (row_count, local_heads, HEAD_DIM)
    query_heads = query_rows.reshape(split_shape)
    table_index = jnp.arange(dwa_table.shape[1])
    onehot = (dwa_slot[:, None] == table_index[None, :]).astype(jnp.float32)
    coefs = jnp.dot(onehot, jnp.transpose(dwa_table), precision=lax.Precision.HIGHEST)
    layer_in = jnp.zeros(queries.shape, jnp.float32)
    extra = jnp.zeros(queries.shape, jnp.float32)
    for index in range(past_outputs.shape[0]):
        stored = past_outputs[index].astype(jnp.float32)
        layer_in = layer_in + coefs[index, 0] * stored
        extra = extra + coefs[index, 1] * stored
    running = jnp.full((local_heads, row_count), -jnp.inf, jnp.float32)
    total = jnp.zeros((local_heads, row_count), jnp.float32)
    accumulated = jnp.zeros(split_shape, jnp.float32)
    state = (running, total, accumulated)
    causal = (jnp.arange(row_count)[:, None] >= jnp.arange(row_count)[None, :])[None, :, :]
    state = block_update(
        state, query_heads, key_rows.reshape(split_shape), value_rows.reshape(split_shape), causal
    )
    position = lax.axis_index("seq")
    current = (key_rows, value_rows)
    for offset in range(1, span_size):
        current = from_behind((current[0], current[1]), "seq", 1)
        far_keys = current[0].reshape(split_shape)
        far_values = current[1].reshape(split_shape)

        def take_block(carry, far_keys=far_keys, far_values=far_values):
            return block_update(carry, query_heads, far_keys, far_values, True)

        def keep_block(carry):
            return carry

        state = lax.cond(position >= offset, take_block, keep_block, state)
    running, total, accumulated = state
    attended = accumulated / jnp.transpose(total)[:, :, None]
    attended = attended.astype(jnp.bfloat16).reshape(row_count, local_heads * HEAD_DIM)
    returned = lax.all_to_all(attended, "uly", split_axis=0, concat_axis=1, tiled=True)
    hidden = layer_in + returned.astype(jnp.float32)
    return (hidden + extra).astype(jnp.bfloat16)


def solution(mesh):
    return jax.shard_map(
        shards,
        mesh=mesh,
        in_specs=(
            P(("rep", "seq", "uly"), None),
            P(("rep", "seq", "uly"), None),
            P(("rep", "seq", "uly"), None),
            P(None, ("rep", "seq", "uly"), None),
            P(),
            P(),
        ),
        out_specs=P(("rep", "seq", "uly"), None),
        check_vma=False,
    )
```

profile of v0, /device:TPU:24, one launch (start us, length us, event | category | flops | bytes accessed | tf_op | source)
XLA Modules:
  0.0 108.4 jit_solution(13092285454462107051)
XLA Ops:
  0.0 1.9 %copy.128 = bf16[16,4,8,512]{3,2,0,1:T(8,128)(2,1)} copy(bf16[16,4,8,512]{3,2,1,0:T(8,128)(2,1)} %bitcast.102) | data formatting | bytes 1048576 | tf_op jit(solution)/shard_map/all_to_all | solution.py:38
  1.9 3.7 %all-to-all-start.1 = ((bf16[128,4,512]{2,0,1:T(8,128)(2,1)}), bf16[128,4,512]{2,0,1:T(8,128)(2,1)S(1)}, u32[]{:S(2)}, u32[]{:S(2)}) async-start(bf16[128,4,512]{2,0,1:T(8,128)(2,1)} %bitcast.95), calls=%async_computation.1 | async-start | bytes 1048576 | tf_op jit(solution)/shard_map/all_to_all | solution.py:38
  5.7 1.9 %copy.127 = bf16[16,4,8,512]{3,2,0,1:T(8,128)(2,1)} copy(bf16[16,4,8,512]{3,2,1,0:T(8,128)(2,1)} %bitcast.103) | data formatting | bytes 1048576 | tf_op jit(solution)/shard_map/all_to_all | solution.py:39
  7.5 6.1 %all-to-all-done.1 = bf16[128,4,512]{2,0,1:T(8,128)(2,1)S(1)} async-done(((bf16[128,4,512]{2,0,1:T(8,128)(2,1)}), bf16[128,4,512]{2,0,1:T(8,128)(2,1)S(1)}, u32[]{:S(2)}, u32[]{:S(2)}) %all-to-all-start.1) | async-done | bytes 524320 | tf_op jit(solution)/shard_map/all_to_all | solution.py:38
  13.7 3.5 %all-to-all-start.2 = ((bf16[128,4,512]{2,0,1:T(8,128)(2,1)}), bf16[128,4,512]{2,0,1:T(8,128)(2,1)S(1)}, u32[]{:S(2)}, u32[]{:S(2)}) async-start(bf16[128,4,512]{2,0,1:T(8,128)(2,1)} %bitcast.94), calls=%async_computation.2 | async-start | bytes 1048576 | tf_op jit(solution)/shard_map/all_to_all | solution.py:39
  18.5 5.9 %all-to-all-done.2 = bf16[128,4,512]{2,0,1:T(8,128)(2,1)S(1)} async-done(((bf16[128,4,512]{2,0,1:T(8,128)(2,1)}), bf16[128,4,512]{2,0,1:T(8,128)(2,1)S(1)}, u32[]{:S(2)}, u32[]{:S(2)}) %all-to-all-start.2) | async-done | bytes 524320 | tf_op jit(solution)/shard_map/all_to_all | solution.py:39
  26.5 3.5 %all-to-all-start = ((bf16[128,4,512]{2,0,1:T(8,128)(2,1)}), bf16[128,4,512]{2,0,1:T(8,128)(2,1)S(1)}, u32[]{:S(2)}, u32[]{:S(2)}) async-start(bf16[128,4,512]{2,0,1:T(8,128)(2,1)} %bitcast.96), calls=%async_computation | async-start | bytes 1048576 | tf_op jit(solution)/shard_map/all_to_all | solution.py:37
  30.1 6.4 %all-to-all-done = bf16[128,4,512]{2,0,1:T(8,128)(2,1)S(1)} async-done(((bf16[128,4,512]{2,0,1:T(8,128)(2,1)}), bf16[128,4,512]{2,0,1:T(8,128)(2,1)S(1)}, u32[]{:S(2)}, u32[]{:S(2)}) %all-to-all-start) | async-done | bytes 524320 | tf_op jit(solution)/shard_map/all_to_all | solution.py:37
  38.1 7.1 %collective-permute-done.1 = bf16[512,512]{1,0:T(8,128)(2,1)} collective-permute-done((bf16[512,512]{1,0:T(8,128)(2,1)S(1)}, bf16[512,512]{1,0:T(8,128)(2,1)}, u32[]{:S(2)}, u32[]{:S(2)}) %collective-permute-start.1) | collective-permute-done | bytes 524320 | tf_op jit(solution)/shard_map/ppermute | solution.py:12
  47.4 1.9 %copy-done.1 = f32[4,512,512]{1,2,0:T(8,128)} copy-done((f32[4,512,512]{1,2,0:T(8,128)}, f32[4,512,512]{1,2,0:T(8,128)S(1)}, u32[]{:S(2)}) %copy-start.1) | copy-done | bytes 4194328
  50.3 6.1 %collective-permute-done.2 = bf16[512,512]{1,0:T(8,128)(2,1)} collective-permute-done((bf16[512,512]{1,0:T(8,128)(2,1)S(1)}, bf16[512,512]{1,0:T(8,128)(2,1)}, u32[]{:S(2)}, u32[]{:S(2)}) %collective-permute-start.2) | collective-permute-done | bytes 524320 | tf_op jit(solution)/shard_map/ppermute | solution.py:12
  57.7 9.9 %collective-permute-done.3 = bf16[512,512]{1,0:T(8,128)(2,1)} collective-permute-done((bf16[512,512]{1,0:T(8,128)(2,1)}, bf16[512,512]{1,0:T(8,128)(2,1)}, u32[]{:S(2)}, u32[]{:S(2)}) %collective-permute-start.3) | collective-permute-done | bytes 524320 | tf_op jit(solution)/shard_map/ppermute | solution.py:12
  69.1 3.8 %fusion.70 = f32[512,4,128]{2,0,1:T(8,128)S(1)} fusion(f32[4,512,512]{1,2,0:T(8,128)} %copy-done.1, f32[4,512]{1,0:T(4,128)S(1)} %get-tuple-element.157, pred[512,512]{0,1:T(8,128)(4,1)S(1)} %iota_compare_fusion, bf16[512,4,128]{2,1,0:T(4,128)(2,1)S(1)} %reshape.86, f32[512,4]{0,1:T(4,128)S(1)} %get-tuple-element.151), kind=kOutput, calls=%fused_computation.66 | convolution fusion | flops 272891904 | bytes 6045696 | tf_op jit(solution)/shard_map/hqk,khd->qhd/dot_general | solution.py:25
  75.2 2.9 %conditional.3 = ((f32[4,512]{1,0:T(4,128)S(1)}, f32[4,512]{1,0:T(4,128)S(1)}, f32[512,4,128]{2,0,1:T(8,128)S(1)})) conditional(s32[]{:T(128)} %convert_element_type.49, (f32[4,512]{1,0:T(4,128)S(1)}, f32[4,512]{1,0:T(4,128)S(1)}, f32[512,4,128]{2,0,1:T(8,128)S(1)}) %tuple.25, (bf16[512,4,128]{2,1,0:T(4,128)(2,1)S(1)}, ...), branch_computations={%region_2.3_spmd, %region_3.6_spmd} | conditional | flops 545789952 | bytes 16384032 | solution.py:74
  76.7 1.4 %fusion.9 = f32[512,4,128]{2,0,1:T(8,128)S(1)} fusion(f32[4,512,512]{1,2,0:T(8,128)S(1)} %get-tuple-element.144, f32[4,512]{1,0:T(4,128)S(1)} %get-tuple-element.162, f32[512,4,128]{2,0,1:T(8,128)S(1)} %get-tuple-element.65, bf16[512,4,128]{2,1,0:T(4,128)(2,1)S(1)} %get-tuple-element.124, f32[512,4]{0,1:T(4,128)S(1)} %get-tuple-element.137), kind=kOutput, calls=%fused_computation.8 | convolution fusion | flops 272105472 | bytes 6832128 | tf_op jit(solution)/shard_map/cond/branch_1_fun/hqk,khd->qhd/dot_general | solution.py:25
  78.2 5.0 %conditional.4 = ((f32[4,512]{1,0:T(4,128)S(1)}, f32[4,512]{1,0:T(4,128)S(1)}, f32[512,4,128]{2,0,1:T(8,128)S(1)})) conditional(s32[]{:T(128)} %convert_element_type.48, (f32[4,512]{1,0:T(4,128)S(1)}, f32[4,512]{1,0:T(4,128)S(1)}, f32[512,4,128]{2,0,1:T(8,128)S(1)}) %get-tuple-element.175, (bf16[512,512]{1,0:T(8,128)(2,1)}, ...), branch_computations={%region_6.7_spmd, %region_7.10_spmd} | conditional | flops 545789952 | bytes 16384032 | solution.py:74
  78.2 1.8 %multiply_reduce_fusion.1 = (f32[4,512]{1,0:T(4,128)S(1)}, f32[4,512,512]{1,2,0:T(8,128)S(1)}) fusion(bf16[512,4,128]{2,1,0:T(4,128)(2,1)S(1)} %get-tuple-element.126, bf16[512,512]{1,0:T(8,128)(2,1)} %get-tuple-element.69), kind=kOutput, calls=%fused_computation.18 | convolution fusion | flops 270530560 | bytes 5251072 | tf_op jit(solution)/shard_map/cond/branch_1_fun/qhd,khd->hqk/dot_general | solution.py:17
  80.7 2.4 %fusion.27 = f32[512,4,128]{2,0,1:T(8,128)S(1)} fusion(f32[4,512,512]{1,2,0:T(8,128)S(1)} %get-tuple-element.146, f32[4,512]{1,0:T(4,128)S(1)} %get-tuple-element.168, f32[512,4,128]{2,0,1:T(8,128)S(1)} %get-tuple-element.71, f32[512,4]{0,1:T(4,128)S(1)} %get-tuple-element.139, bf16[512,512]{1,0:T(8,128)(2,1)} %get-tuple-element.72), kind=kOutput, calls=%fused_computation.25 | convolution fusion | flops 272105472 | bytes 6832128 | tf_op jit(solution)/shard_map/cond/branch_1_fun/hqk,khd->qhd/dot_general | solution.py:25
  83.1 4.8 %collective-permute-done.5 = bf16[512,512]{1,0:T(8,128)(2,1)} collective-permute-done((bf16[512,512]{1,0:T(8,128)(2,1)}, bf16[512,512]{1,0:T(8,128)(2,1)}, u32[]{:S(2)}, u32[]{:S(2)}) %collective-permute-start.5) | collective-permute-done | bytes 524320 | tf_op jit(solution)/shard_map/ppermute | solution.py:12
  87.9 3.9 %conditional.5 = ((f32[4,512]{1,0:T(4,128)S(1)}, f32[512,4,128]{2,0,1:T(8,128)S(1)})) conditional(s32[]{:T(128)} %convert_element_type.47, (f32[4,512]{1,0:T(4,128)S(1)}, f32[512,4,128]{2,0,1:T(8,128)S(1)}) %tuple.28, (bf16[512,512]{1,0:T(8,128)(2,1)S(1)}, bf16[512,4,128]{2,1,0:T(4,128)(2,1)S(1)}, f32[4,512]{1,0:T(4,128)S(1)}, ...), branch_computations={%region_10.11_spmd, %region_11.14_spmd} | conditional | flops 545789952 | bytes 16367640 | solution.py:74
  89.4 2.4 %fusion.47 = f32[512,4,128]{2,0,1:T(8,128)S(1)} fusion(f32[4,512,512]{1,2,0:T(8,128)S(1)} %get-tuple-element.148, f32[4,512]{1,0:T(4,128)S(1)} %get-tuple-element.142, f32[512,4,128]{2,0,1:T(8,128)S(1)} %get-tuple-element.77, f32[512,4]{0,1:T(4,128)S(1)} %get-tuple-element.141, bf16[512,512]{1,0:T(8,128)(2,1)} %get-tuple-element.78), kind=kOutput, calls=%fused_computation.44 | convolution fusion | flops 272105472 | bytes 6832128 | tf_op jit(solution)/shard_map/cond/branch_1_fun/hqk,khd->qhd/dot_general | solution.py:25
  93.6 3.9 %all-to-all-start.3 = ((bf16[4,128,512]{2,1,0:T(8,128)(2,1)}), bf16[4,128,512]{2,1,0:T(8,128)(2,1)S(1)}, u32[]{:S(2)}, u32[]{:S(2)}) async-start(bf16[4,128,512]{2,1,0:T(8,128)(2,1)} %all_to_all.61), calls=%async_computation.3 | async-start | bytes 1048576 | tf_op jit(solution)/shard_map/all_to_all | solution.py:78
  99.0 5.0 %all-to-all-done.3 = bf16[4,128,512]{2,1,0:T(8,128)(2,1)S(1)} async-done(((bf16[4,128,512]{2,1,0:T(8,128)(2,1)}), bf16[4,128,512]{2,1,0:T(8,128)(2,1)S(1)}, u32[]{:S(2)}, u32[]{:S(2)}) %all-to-all-start.3) | async-done | bytes 524320 | tf_op jit(solution)/shard_map/all_to_all | solution.py:78
  104.5 2.8 %fusion.77 = bf16[128,2048]{0,1:T(8,128)(2,1)S(1)} fusion(bf16[1,128,2048]{1,2,0:T(8,128)(2,1)S(1)} %copy.67, bf16[1,128,2048]{1,2,0:T(8,128)(2,1)S(1)} %copy.68, f32[128,4,512]{0,2,1:T(8,128)S(1)} %copy.61, f32[]{:T(128)} %bitcast.20, f32[]{:T(128)} %bitcast.19, f32[]{:T(128)} %bitcast.7, f32[]{:T(128)} %bitcast.6), kind=kLoop, calls=%fused_computation.75 | loop fusion | flops 2883584 | bytes 2621456 | tf_op jit(solution)/shard_map/convert_element_type | solution.py:80
  (53 shorter events, 21.6 us)
Async XLA Ops:
  0.0 98.2 %copy-start = (f32[2,64]{1,0:T(2,128)S(1)}, f32[2,64]{1,0:T(2,128)}, u32[]{:S(2)}) copy-start(f32[2,64]{1,0:T(2,128)} %param.17) | copy-start | bytes 1540
  0.0 25.6 %copy-start.3 = (bf16[128,2048]{1,0:T(8,128)(2,1)S(1)}, bf16[128,2048]{1,0:T(8,128)(2,1)}, u32[]{:S(2)}) copy-start(bf16[128,2048]{1,0:T(8,128)(2,1)} %param.12) | copy-start | bytes 1572868
  1.9 11.7 %all-to-all-start.1 = ((bf16[128,4,512]{2,0,1:T(8,128)(2,1)}), bf16[128,4,512]{2,0,1:T(8,128)(2,1)S(1)}, u32[]{:S(2)}, u32[]{:S(2)}) async-start(bf16[128,4,512]{2,0,1:T(8,128)(2,1)} %bitcast.95), calls=%async_computation.1 | async-start | bytes 1048576 | tf_op jit(solution)/shard_map/all_to_all | solution.py:38
  13.7 10.7 %all-to-all-start.2 = ((bf16[128,4,512]{2,0,1:T(8,128)(2,1)}), bf16[128,4,512]{2,0,1:T(8,128)(2,1)S(1)}, u32[]{:S(2)}, u32[]{:S(2)}) async-start(bf16[128,4,512]{2,0,1:T(8,128)(2,1)} %bitcast.94), calls=%async_computation.2 | async-start | bytes 1048576 | tf_op jit(solution)/shard_map/all_to_all | solution.py:39
  17.2 19.6 %collective-permute-start = (bf16[512,512]{1,0:T(8,128)(2,1)S(1)}, bf16[512,512]{1,0:T(8,128)(2,1)S(1)}, u32[]{:S(2)}, u32[]{:S(2)}) collective-permute-start(bf16[512,512]{1,0:T(8,128)(2,1)S(1)} %bitcast.99), channel_id=1, source_target_pairs={{0,8},{8,16},{16,24},{1,9},{9,17},{17,25},{2,10},{10,18},{18,26},{... | collective-permute-start | bytes 1572872 | tf_op jit(solution)/shard_map/ppermute | solution.py:12
  24.3 20.9 %collective-permute-start.1 = (bf16[512,512]{1,0:T(8,128)(2,1)S(1)}, bf16[512,512]{1,0:T(8,128)(2,1)}, u32[]{:S(2)}, u32[]{:S(2)}) collective-permute-start(bf16[512,512]{1,0:T(8,128)(2,1)S(1)} %bitcast.97), channel_id=1, source_target_pairs={{0,8},{8,16},{16,24},{1,9},{9,17},{17,25},{2,10},{10,18},{18,26},{... | collective-permute-start | bytes 1572872 | tf_op jit(solution)/shard_map/ppermute | solution.py:12
  26.5 10.0 %all-to-all-start = ((bf16[128,4,512]{2,0,1:T(8,128)(2,1)}), bf16[128,4,512]{2,0,1:T(8,128)(2,1)S(1)}, u32[]{:S(2)}, u32[]{:S(2)}) async-start(bf16[128,4,512]{2,0,1:T(8,128)(2,1)} %bitcast.96), calls=%async_computation | async-start | bytes 1048576 | tf_op jit(solution)/shard_map/all_to_all | solution.py:37
  36.8 13.5 %copy-start.4 = (bf16[512,512]{1,0:T(8,128)(2,1)}, bf16[512,512]{1,0:T(8,128)(2,1)S(1)}, u32[]{:S(2)}) copy-start(bf16[512,512]{1,0:T(8,128)(2,1)S(1)} %collective-permute-done) | copy-start | bytes 1572868
  36.8 19.6 %collective-permute-start.2 = (bf16[512,512]{1,0:T(8,128)(2,1)S(1)}, bf16[512,512]{1,0:T(8,128)(2,1)}, u32[]{:S(2)}, u32[]{:S(2)}) collective-permute-start(bf16[512,512]{1,0:T(8,128)(2,1)S(1)} %collective-permute-done), channel_id=1, source_target_pairs={{0,8},{8,16},{16,24},{1,9},{9,17},{17,25},{2,10},{10,18},{18,26},{... | collective-permute-start | bytes 1572872 | tf_op jit(solution)/shard_map/ppermute | solution.py:12
  45.2 22.5 %collective-permute-start.3 = (bf16[512,512]{1,0:T(8,128)(2,1)}, bf16[512,512]{1,0:T(8,128)(2,1)}, u32[]{:S(2)}, u32[]{:S(2)}) collective-permute-start(bf16[512,512]{1,0:T(8,128)(2,1)} %collective-permute-done.1), channel_id=1, source_target_pairs={{0,8},{8,16},{16,24},{1,9},{9,17},{17,25},{2,10},{10,18},{18,26},{... | collective-permute-start | bytes 1572872 | tf_op jit(solution)/shard_map/ppermute | solution.py:12
  47.4 1.9 %copy-start.1 = (f32[4,512,512]{1,2,0:T(8,128)}, f32[4,512,512]{1,2,0:T(8,128)S(1)}, u32[]{:S(2)}) copy-start(f32[4,512,512]{1,2,0:T(8,128)S(1)} %get-tuple-element.158) | copy-start | bytes 12582916
  56.4 26.7 %collective-permute-start.4 = (bf16[512,512]{1,0:T(8,128)(2,1)}, bf16[512,512]{1,0:T(8,128)(2,1)S(1)}, u32[]{:S(2)}, u32[]{:S(2)}) collective-permute-start(bf16[512,512]{1,0:T(8,128)(2,1)} %collective-permute-done.2), channel_id=1, source_target_pairs={{0,8},{8,16},{16,24},{1,9},{9,17},{17,25},{2,10},{10,18},{18,26},{... | collective-permute-start | bytes 1572872 | tf_op jit(solution)/shard_map/ppermute | solution.py:12
  67.7 20.3 %collective-permute-start.5 = (bf16[512,512]{1,0:T(8,128)(2,1)}, bf16[512,512]{1,0:T(8,128)(2,1)}, u32[]{:S(2)}, u32[]{:S(2)}) collective-permute-start(bf16[512,512]{1,0:T(8,128)(2,1)} %collective-permute-done.3), channel_id=1, source_target_pairs={{0,8},{8,16},{16,24},{1,9},{9,17},{17,25},{2,10},{10,18},{18,26},{... | collective-permute-start | bytes 1572872 | tf_op jit(solution)/shard_map/ppermute | solution.py:12
  91.8 5.7 %copy-start.2 = (bf16[2,128,2048]{2,1,0:T(8,128)(2,1)S(1)}, bf16[2,128,2048]{2,1,0:T(8,128)(2,1)}, u32[]{:S(2)}) copy-start(bf16[2,128,2048]{2,1,0:T(8,128)(2,1)} %param.15) | copy-start | bytes 3145732
  91.9 6.3 %copy-start.5 = (s32[2]{0:T(128)S(1)}, s32[2]{0:T(128)}, u32[]{:S(2)}) copy-start(s32[2]{0:T(128)} %param.16) | copy-start | bytes 28
  93.6 10.4 %all-to-all-start.3 = ((bf16[4,128,512]{2,1,0:T(8,128)(2,1)}), bf16[4,128,512]{2,1,0:T(8,128)(2,1)S(1)}, u32[]{:S(2)}, u32[]{:S(2)}) async-start(bf16[4,128,512]{2,1,0:T(8,128)(2,1)} %all_to_all.61), calls=%async_computation.3 | async-start | bytes 1048576 | tf_op jit(solution)/shard_map/all_to_all | solution.py:78
where the time goes:
time: 109 us; the launch traced here: 108 us
  waiting for transfers between devices  51.5 us (47%)
  starting transfers between devices  22.2 us (20%)
  matrix products  14.4 us (13%)
  local copies, waits for them, and re-layouts  13.4 us (12%)
  other arithmetic  6.49 us (6%)
    ppermute x6, waiting for transfers between devices, from_behind(): return lax.ppermute(block, axis, route)  28 us
    dot_general x4, matrix products, block_update(): jnp.einsum('hqk,khd->qhd', weights, value_heads, preferred_element_type=j...  10.1 us
    ppermute x6, starting transfers between devices, from_behind(): return lax.ppermute(block, axis, route)  7.71 us
    all_to_all x1, waiting for transfers between devices, shards(): lax.all_to_all(queries, 'uly', split_axis=1, concat_axis=0, tiled=True)  6.45 us
    all_to_all x1, waiting for transfers between devices, shards(): lax.all_to_all(keys, 'uly', split_axis=1, concat_axis=0, tiled=True)  6.15 us
    all_to_all x1, waiting for transfers between devices, shards(): lax.all_to_all(values, 'uly', split_axis=1, concat_axis=0, tiled=True)  5.88 us
    all_to_all x1, waiting for transfers between devices, shards(): lax.all_to_all(attended, 'uly', split_axis=0, concat_axis=1, tiled=True)  5.04 us
    dot_general x4, matrix products, block_update(): jnp.einsum('qhd,khd->hqk', query_heads, key_heads, preferred_element_type...  4.16 us
  transfers between devices with their start and end apart: 10, of which 8 were waited for; matrix products, arithmetic and copies ran while one was open for 19% of the time, Pallas kernels for 0%

commit v1 on v0

--- a/solution.py
+++ b/solution.py
@@ -1,9 +1,17 @@
+import functools
+
 import jax
 import jax.numpy as jnp
 from jax import lax
+from jax.experimental import pallas as pl
+from jax.experimental.pallas import tpu as pltpu
 from jax.sharding import PartitionSpec as P
 
 HEAD_DIM = 128
+SPAN = 4
+CHUNKS = 2
+STAT_ROWS = 16
+SCALE = 1.4426950408889634 / HEAD_DIM**0.5
 
 
 def from_behind(block, axis, distance):
@@ -27,10 +35,10 @@
     return (new_max, total, accumulated)
 
 
-def shards(queries, keys, values, past_outputs, dwa_slot, dwa_table):
+def ring_shards(queries, keys, values, past_outputs, dwa_slot, dwa_table):
     n_uly = lax.axis_size("uly")
     n_seq = lax.axis_size("seq")
-    span_size = min(4, n_seq)
+    span_size = min(SPAN, n_seq)
     features = queries.shape[1]
     local_heads = features // n_uly // HEAD_DIM
     query_rows, key_rows, value_rows = (
@@ -80,6 +88,182 @@
     return (hidden + extra).astype(jnp.bfloat16)
 
 
+def pack_kernel(where, q, k, v, *outs):
+    width = outs[0].shape[2]
+    n = len(outs) // CHUNKS
+    for s in range(n):
+        for c in range(CHUNKS):
+            start = pl.multiple_of((where[1] ^ s) * (width * CHUNKS) + c * width, HEAD_DIM)
+            for t, ref in enumerate((q, k, v)):
+                outs[c * n + s][t] = ref[:, pl.ds(start, width)]
+
+
+def attend(query, blocks, allowed):
+    scores = []
+    for key, _ in blocks:
+        scores.append(lax.dot_general(key, query, (((1,), (1,)), ((), ())), preferred_element_type=jnp.float32))
+    if allowed is not None:
+        scores[-1] = jnp.where(allowed, scores[-1], -jnp.inf)
+    top = jnp.max(scores[0], axis=0, keepdims=True)
+    for other in scores[1:]:
+        top = jnp.maximum(top, jnp.max(other, axis=0, keepdims=True))
+    total, summed = 0.0, 0.0
+    for score, (_, value) in zip(scores, blocks):
+        prob = jnp.exp2((score - top) * SCALE)
+        total = total + jnp.sum(prob, axis=0, keepdims=True)
+        summed = summed + lax.dot_general(
+            value, prob.astype(jnp.bfloat16), (((0,), (0,)), ((), ())), preferred_element_type=jnp.float32
+        )
+    return summed / total, top * SCALE + jnp.log2(total)
+
+
+def attention_kernel(part, where, q, kv, far, qa, qb, own, lse, ra, rb):
+    z, u = where[0], where[1]
+    rows = q.shape[0]
+    spot = lambda axis: lax.broadcasted_iota(jnp.int32, (rows, rows), axis)
+    place = lambda i: (((i // part) ^ u) * part) + i % part
+    near = (kv[0], kv[1])
+    odd = z % 2 == 1
+
+    def put(result):
+        own[0] = result[0]
+        lse[0] = jnp.broadcast_to(result[1], lse.shape[1:])
+
+    def send(out, result):
+        out[0, :HEAD_DIM] = result[0].astype(jnp.bfloat16)
+        high = result[1].astype(jnp.bfloat16).astype(jnp.float32)
+        middle = (result[1] - high).astype(jnp.bfloat16).astype(jnp.float32)
+        low = result[1] - high - middle
+        row = lax.broadcasted_iota(jnp.int32, (STAT_ROWS, rows), 0)
+        stats = jnp.where(row == 0, high, jnp.where(row == 1, middle, jnp.where(row == 2, low, 0.0)))
+        out[0, HEAD_DIM:] = stats.astype(jnp.bfloat16)
+
+    @pl.when(z == 1)
+    def _():
+        send(rb, attend(qb[...], [(far[0], far[1]), near], None))
+        send(ra, attend(qa[...], [(far[0], far[1]), near], None))
+
+    @pl.when(odd)
+    def _():
+        allowed = place(spot(1)) >= place(spot(0))
+        put(attend(q[...], [(far[0], far[1]), near], allowed))
+
+    @pl.when(jnp.logical_not(odd))
+    def _():
+        allowed = place(spot(1)) >= place(spot(0))
+        put(attend(q[...], [near], allowed))
+
+
+def merge_kernel(where, own, lse, ra, rb, *outs):
+    z = where[0]
+
+    def write(result):
+        tokens = jnp.transpose(result).astype(jnp.bfloat16)
+        rows = outs[0].shape[0]
+        for s, out in enumerate(outs):
+            out[...] = tokens[s * rows : (s + 1) * rows]
+
+    def merged(ref):
+        stats = ref[0, HEAD_DIM:].astype(jnp.float32)
+        other = stats[0:1] + stats[1:2] + stats[2:3]
+        mine = lse[0, 0:1]
+        top = jnp.maximum(mine, other)
+        w_mine, w_other = jnp.exp2(mine - top), jnp.exp2(other - top)
+        scale = 1.0 / (w_mine + w_other)
+        write(own[0] * (w_mine * scale) + ref[0, :HEAD_DIM].astype(jnp.float32) * (w_other * scale))
+
+    pl.when(z < 2)(lambda: write(own[0]))
+    pl.when(z == 2)(lambda: merged(ra))
+    pl.when(z == 3)(lambda: merged(rb))
+
+
+def mix_kernel(where, slot, table, past, *refs):
+    out, parts = refs[-1], refs[:-1]
+    n = len(parts) // CHUNKS
+    width = parts[0].shape[1]
+    coefs = [table[0, slot[p]] + table[1, slot[p]] for p in range(past.shape[0])]
+    for s in range(n):
+        for c in range(CHUNKS):
+            cols = pl.ds(pl.multiple_of((where[1] ^ s) * (width * CHUNKS) + c * width, HEAD_DIM), width)
+            acc = parts[c * n + s][...].astype(jnp.float32)
+            for p, coef in enumerate(coefs):
+                acc = acc + coef * past[p, :, cols].astype(jnp.float32)
+            out[:, cols] = acc.astype(jnp.bfloat16)
+
+
+SMEM = pl.BlockSpec(memory_space=pltpu.SMEM)
+VMEM = pl.BlockSpec(memory_space=pltpu.VMEM)
+
+
+def shards(queries, keys, values, past_outputs, dwa_slot, dwa_table):
+    n_uly, n_seq = lax.axis_size("uly"), lax.axis_size("seq")
+    rows, features = queries.shape
+    heads = features // n_uly // HEAD_DIM
+    if n_seq != 4 or n_uly & (n_uly - 1) or heads % CHUNKS:
+        return ring_shards(queries, keys, values, past_outputs, dwa_slot, dwa_table)
+    where = jnp.stack([lax.axis_index("seq"), lax.axis_index("uly")]).astype(jnp.int32)
+    hc = heads // CHUNKS
+    width = hc * HEAD_DIM
+    block = n_uly * rows
+    bf16, f32 = jnp.bfloat16, jnp.float32
+    shape = jax.ShapeDtypeStruct
+
+    def swap(array, s):
+        return lax.ppermute(array, "uly", [(i, i ^ s) for i in range(n_uly)])
+
+    packed = pl.pallas_call(
+        pack_kernel,
+        in_specs=[SMEM, VMEM, VMEM, VMEM],
+        out_specs=[VMEM] * (CHUNKS * n_uly),
+        out_shape=[shape((3, rows, width), bf16)] * (CHUNKS * n_uly),
+    )(where, queries, keys, values)
+
+    def head_block(count):
+        return pl.BlockSpec((count, block, HEAD_DIM), lambda h: (0, 0, h))
+
+    flat = pl.BlockSpec((block, HEAD_DIM), lambda h: (0, h))
+
+    def per_head(size):
+        return pl.BlockSpec((1, size, block), lambda h: (h, 0, 0))
+
+    arrived = [[packed[c * n_uly + s] if s == 0 else swap(packed[c * n_uly + s], s) for s in range(n_uly)] for c in range(CHUNKS)]
+    results = []
+    for c in range(CHUNKS):
+        q = jnp.concatenate([a[0] for a in arrived[c]], axis=0)
+        kv = jnp.concatenate([a[1:3] for a in arrived[c]], axis=1)
+        qb = lax.ppermute(q, "seq", [(3, 1)])
+        qa = lax.ppermute(q, "seq", [(2, 1)])
+        far = lax.ppermute(kv, "seq", [(0, 1), (2, 3)])
+        own, lse, ra, rb = pl.pallas_call(
+            functools.partial(attention_kernel, rows),
+            grid=(hc,),
+            in_specs=[SMEM, flat, head_block(2), head_block(2), flat, flat],
+            out_specs=[per_head(HEAD_DIM), per_head(8), per_head(HEAD_DIM + STAT_ROWS), per_head(HEAD_DIM + STAT_ROWS)],
+            out_shape=[
+                shape((hc, HEAD_DIM, block), f32),
+                shape((hc, 8, block), f32),
+                shape((hc, HEAD_DIM + STAT_ROWS, block), bf16),
+                shape((hc, HEAD_DIM + STAT_ROWS, block), bf16),
+            ],
+        )(where, q, kv, far, qa, qb)
+        rb = lax.ppermute(rb, "seq", [(1, 3)])
+        ra = lax.ppermute(ra, "seq", [(1, 2)])
+        outs = pl.pallas_call(
+            merge_kernel,
+            grid=(hc,),
+            in_specs=[SMEM, per_head(HEAD_DIM), per_head(8), per_head(HEAD_DIM + STAT_ROWS), per_head(HEAD_DIM + STAT_ROWS)],
+            out_specs=[pl.BlockSpec((rows, HEAD_DIM), lambda h: (0, h))] * n_uly,
+            out_shape=[shape((rows, width), bf16)] * n_uly,
+        )(where, own, lse, ra, rb)
+        results += [out if s == 0 else swap(out, s) for s, out in enumerate(outs)]
+    return pl.pallas_call(
+        mix_kernel,
+        in_specs=[SMEM, SMEM, SMEM] + [VMEM] * (1 + len(results)),
+        out_specs=VMEM,
+        out_shape=shape((rows, features), bf16),
+    )(where, dwa_slot, dwa_table, past_outputs, *results)
+
+
 def solution(mesh):
     return jax.shard_map(
         shards,

time: 109 us -> 86.8 us (0.80)
  waiting for transfers between devices: 51.5 us -> 26.3 us
  Pallas kernels: 0 us -> 18 us
  matrix products: 14.4 us -> 0 us
  starting transfers between devices: 22.2 us -> 33.9 us
  local copies, waits for them, and re-layouts: 13.4 us -> 6.79 us
  other arithmetic: 6.49 us -> 0.73 us
    ppermute x6 -> x22, starting transfers between devices: 7.71 us -> 33.9 us  [the longest x12 14.8 us: swap(): return lax.ppermute(array, 'uly', [(i, i ^ s) for i in range(n_uly)])]
    all_to_all x4 -> x0, waiting for transfers between devices: 23.5 us -> none  [the longest x1 6.45 us: shards(): lax.all_to_all(queries, 'uly', split_axis=1, concat_axis=0, tiled=True)]
    pallas_call x0 -> x6, Pallas kernels: none -> 18 us  [the longest x2 8.61 us: shards(): pl.pallas_call(functools.partial(attention_kernel, rows), grid=(hc,), in_...]
    all_to_all x4 -> x0, starting transfers between devices: 14.5 us -> none  [the longest x1 3.87 us: shards(): lax.all_to_all(attended, 'uly', split_axis=0, concat_axis=1, tiled=True)]
    dot_general x9 -> x0, matrix products: 14.4 us -> none  [the longest x4 10.1 us: block_update(): jnp.einsum('hqk,khd->qhd', weights, value_heads, preferred_element_type=j...]
    all_to_all x4 -> x0, local copies, waits for them, and re-layouts: 5.65 us -> none  [the longest x1 1.94 us: shards(): lax.all_to_all(keys, 'uly', split_axis=1, concat_axis=0, tiled=True)]
    convert_element_type x3 -> x0, other arithmetic: 3.27 us -> none  [the longest x1 2.81 us: shards(): return (hidden + extra).astype(jnp.bfloat16)]
    reduce_sum x4 -> x0, other arithmetic: 3.04 us -> none  [block_update(): total = total * factor + jnp.sum(prob, axis=2)]
  transfers between devices with their start and end apart: 10 -> 22, of which waited for: 8 -> 10; matrix products, arithmetic and copies ran while one was open for 19% -> 2% of each run, Pallas kernels for 0% -> 15%
where the time goes in v1:
time: 86.8 us; the launch traced here: 86.2 us
  starting transfers between devices  33.9 us (39%)
  waiting for transfers between devices  26.3 us (30%)
  Pallas kernels  18 us (21%)
  local copies, waits for them, and re-layouts  6.79 us (8%)
    ppermute x12, starting transfers between devices, swap(): return lax.ppermute(array, 'uly', [(i, i ^ s) for i in range(n_uly)])  14.8 us
    ppermute x2, starting transfers between devices, shards(): qb = lax.ppermute(q, 'seq', [(3, 1)])  11.3 us
    ppermute x2, waiting for transfers between devices, shards(): rb = lax.ppermute(rb, 'seq', [(1, 3)])  10.5 us
    ppermute x12, waiting for transfers between devices, swap(): return lax.ppermute(array, 'uly', [(i, i ^ s) for i in range(n_uly)])  8.98 us
    pallas_call x2, Pallas kernels, shards(): pl.pallas_call(functools.partial(attention_kernel, rows), grid=(hc,), in_...  8.61 us
    ppermute x2, waiting for transfers between devices, shards(): far = lax.ppermute(kv, 'seq', [(0, 1), (2, 3)])  6.78 us
    pallas_call x2, Pallas kernels, shards(): pl.pallas_call(merge_kernel, grid=(hc,), in_specs=[SMEM, per_head(HEAD_DI...  4.26 us
    unnamed x46, local copies, waits for them, and re-layouts  3.97 us
  transfers between devices with their start and end apart: 22, of which 10 were waited for; matrix products, arithmetic and copies ran while one was open for 2% of the time, Pallas kernels for 15%

profile of v1, /device:TPU:24, one launch (start us, length us, event | category | flops | bytes accessed | tf_op | source)
XLA Modules:
  0.0 86.2 jit_solution(7733681269379593208)
XLA Ops:
  0.6 2.7 %shard_map.64 = (bf16[3,128,256]{2,1,0:T(8,128)(2,1)}, bf16[3,128,256]{2,1,0:T(8,128)(2,1)}, bf16[3,128,256]{2,1,0:T(8,128)(2,1)}, bf16[3,128,256]{2,1,0:T(8,128...) custom-call(s32[2]{0:T(128)} %pad_add_fusion.where, ...), custom_call_target="tpu_custom_call" | custom-call | tf_op jit(solution)/shard_map/pallas_call | solution.py:214
  3.3 2.4 %collective-permute-start.13 = (bf16[3,128,256]{2,1,0:T(8,128)(2,1)}, bf16[3,128,256]{2,1,0:T(8,128)(2,1)S(1)}, u32[]{:S(2)}, u32[]{:S(2)}) collective-permute-start(bf16[3,128,256]{2,1,0:T(8,128)(2,1)} %get-tuple-element.44), channel_id=1, source_target_pairs={{0,6},{2,4},{4,2},{6,0},{1,7},{3,5},{5,3},{7,1},{8,14},{10,12},{12... | collective-permute-start | bytes 589832 | tf_op jit(solution)/shard_map/ppermute | solution.py:212
  6.8 2.4 %collective-permute-start.2 = (bf16[3,128,256]{2,1,0:T(8,128)(2,1)}, bf16[3,128,256]{2,1,0:T(8,128)(2,1)S(1)}, u32[]{:S(2)}, u32[]{:S(2)}) collective-permute-start(bf16[3,128,256]{2,1,0:T(8,128)(2,1)} %get-tuple-element.32), channel_id=1, source_target_pairs={{0,6},{2,4},{4,2},{6,0},{1,7},{3,5},{5,3},{7,1},{8,14},{10,12},{12... | collective-permute-start | bytes 589832 | tf_op jit(solution)/shard_map/ppermute | solution.py:212
  13.8 2.8 %collective-permute-done.12 = bf16[3,128,256]{2,1,0:T(8,128)(2,1)S(1)} collective-permute-done((bf16[3,128,256]{2,1,0:T(8,128)(2,1)}, bf16[3,128,256]{2,1,0:T(8,128)(2,1)S(1)}, u32[]{:S(2)}, u32[]{:S(2)}) %collective-permute-start.12) | collective-permute-done | bytes 196640 | tf_op jit(solution)/shard_map/ppermute | solution.py:212
  17.3 2.9 %collective-permute-start.16 = (bf16[512,256]{1,0:T(8,128)(2,1)S(1)}, bf16[512,256]{1,0:T(8,128)(2,1)S(1)}, u32[]{:S(2)}, u32[]{:S(2)}) collective-permute-start(bf16[512,256]{1,0:T(8,128)(2,1)S(1)} %pad_maximum_fusion.3.q), channel_id=1, source_target_pairs={{24,8},{25,9},{26,10},{27,11},{28,12},{29,13},{30,14},{31,15}} | collective-permute-start | bytes 786440 | tf_op jit(solution)/shard_map/ppermute | solution.py:234
  21.2 2.6 %collective-permute-done = bf16[3,128,256]{2,1,0:T(8,128)(2,1)S(1)} collective-permute-done((bf16[3,128,256]{2,1,0:T(8,128)(2,1)S(1)}, bf16[3,128,256]{2,1,0:T(8,128)(2,1)S(1)}, u32[]{:S(2)}, u32[]{:S(2)}) %collective-permute-start) | collective-permute-done | bytes 196640 | tf_op jit(solution)/shard_map/ppermute | solution.py:212
  25.3 1.3 %collective-permute-start.3 = (bf16[2,512,256]{2,1,0:T(8,128)(2,1)S(1)}, bf16[2,512,256]{2,1,0:T(8,128)(2,1)S(1)}, u32[]{:S(2)}, u32[]{:S(2)}) collective-permute-start(bf16[2,512,256]{2,1,0:T(8,128)(2,1)S(1)} %pad_maximum_fusion.kv), channel_id=1, source_target_pairs={{0,8},{16,24},{1,9},{17,25},{2,10},{18,26},{3,11},{19,27},{4,12},{... | collective-permute-start | bytes 1572872 | tf_op jit(solution)/shard_map/ppermute | solution.py:236
  27.4 8.5 %collective-permute-start.5 = (bf16[512,256]{1,0:T(8,128)(2,1)S(1)}, bf16[512,256]{1,0:T(8,128)(2,1)}, u32[]{:S(2)}, u32[]{:S(2)}) collective-permute-start(bf16[512,256]{1,0:T(8,128)(2,1)S(1)} %pad_maximum_fusion.2.q), channel_id=1, source_target_pairs={{24,8},{25,9},{26,10},{27,11},{28,12},{29,13},{30,14},{31,15}} | collective-permute-start | bytes 786440 | tf_op jit(solution)/shard_map/ppermute | solution.py:234
  35.9 4.7 %collective-permute-done.14.far = bf16[2,512,256]{2,1,0:T(8,128)(2,1)S(1)} collective-permute-done((bf16[2,512,256]{2,1,0:T(8,128)(2,1)S(1)}, bf16[2,512,256]{2,1,0:T(8,128)(2,1)S(1)}, u32[]{:S(2)}, u32[]{:S(2)}) %collective-permute-start.14) | collective-permute-done | bytes 524320 | tf_op jit(solution)/shard_map/ppermute | solution.py:236
  41.4 4.3 %shard_map.67 = (f32[2,128,512]{2,1,0:T(8,128)}, f32[2,8,512]{2,1,0:T(8,128)}, bf16[2,144,512]{2,1,0:T(8,128)(2,1)}, bf16[2,144,512]{2,1,0:T(8,128)(2,1)}) custom-call(s32[2]{0:T(128)} %pad_add_fusion.where, bf16[512,256]{1,0:T(8,128)(2,1)} %copy-done.2, bf16[2,512,256]{2,1,0:T(8,128)(2,1)} %copy-done, bf16[2,512,256]{2,1,0:T(8,128)(2,1)} %copy-done.5, ...), custom_call_target="tpu_custom_call" | custom-call | tf_op jit(solution)/shard_map/pallas_call | solution.py:237
  46.4 1.3 %collective-permute-start.18 = (bf16[2,144,512]{2,1,0:T(8,128)(2,1)}, bf16[2,144,512]{2,1,0:T(8,128)(2,1)S(1)}, u32[]{:S(2)}, u32[]{:S(2)}) collective-permute-start(bf16[2,144,512]{2,1,0:T(8,128)(2,1)} %get-tuple-element.48), channel_id=1, source_target_pairs={{8,24},{9,25},{10,26},{11,27},{12,28},{13,29},{14,30},{15,31}} | collective-permute-start | bytes 884744 | tf_op jit(solution)/shard_map/ppermute | solution.py:249
  47.7 2.1 %collective-permute-done.3.far = bf16[2,512,256]{2,1,0:T(8,128)(2,1)S(1)} collective-permute-done((bf16[2,512,256]{2,1,0:T(8,128)(2,1)S(1)}, bf16[2,512,256]{2,1,0:T(8,128)(2,1)S(1)}, u32[]{:S(2)}, u32[]{:S(2)}) %collective-permute-start.3) | collective-permute-done | bytes 524320 | tf_op jit(solution)/shard_map/ppermute | solution.py:236
  50.6 4.3 %shard_map.65 = (f32[2,128,512]{2,1,0:T(8,128)}, f32[2,8,512]{2,1,0:T(8,128)}, bf16[2,144,512]{2,1,0:T(8,128)(2,1)}, bf16[2,144,512]{2,1,0:T(8,128)(2,1)}) custom-call(s32[2]{0:T(128)} %pad_add_fusion.where, bf16[512,256]{1,0:T(8,128)(2,1)} %copy-done.3, bf16[2,512,256]{2,1,0:T(8,128)(2,1)} %copy-done.1, bf16[2,512,256]{2,1,0:T(8,128)(2,1)} %copy-done.4, ...), custom_call_target="tpu_custom_call" | custom-call | tf_op jit(solution)/shard_map/pallas_call | solution.py:237
  55.6 1.3 %collective-permute-start.7 = (bf16[2,144,512]{2,1,0:T(8,128)(2,1)}, bf16[2,144,512]{2,1,0:T(8,128)(2,1)S(1)}, u32[]{:S(2)}, u32[]{:S(2)}) collective-permute-start(bf16[2,144,512]{2,1,0:T(8,128)(2,1)} %get-tuple-element.36), channel_id=1, source_target_pairs={{8,24},{9,25},{10,26},{11,27},{12,28},{13,29},{14,30},{15,31}} | collective-permute-start | bytes 884744 | tf_op jit(solution)/shard_map/ppermute | solution.py:249
  56.9 4.4 %collective-permute-done.18.rb = bf16[2,144,512]{2,1,0:T(8,128)(2,1)S(1)} collective-permute-done((bf16[2,144,512]{2,1,0:T(8,128)(2,1)}, bf16[2,144,512]{2,1,0:T(8,128)(2,1)S(1)}, u32[]{:S(2)}, u32[]{:S(2)}) %collective-permute-start.18) | collective-permute-done | bytes 294944 | tf_op jit(solution)/shard_map/ppermute | solution.py:249
  62.0 2.1 %shard_map.68 = (bf16[128,256]{1,0:T(8,128)(2,1)}, bf16[128,256]{1,0:T(8,128)(2,1)}, bf16[128,256]{1,0:T(8,128)(2,1)}, bf16[128,256]{1,0:T(8,128)(2,1)}) custom-call(s32[2]{0:T(128)} %pad_add_fusion.where, f32[2,128,512]{2,1,0:T(8,128)} %get-tuple-element.45.own, f32[2,8,512]{2,1,0:T(8,128)} %get-tuple-element.46.lse, bf16[2,144,512]{2,1,0:T(8,128)(2,1)} %copy-done.9, ...), custom_call_target="tpu_custom_call" | custom-call | tf_op jit(solution)/shard_map/pallas_call | solution.py:251
  64.2 1.6 %collective-permute-start.19 = (bf16[128,256]{1,0:T(8,128)(2,1)}, bf16[128,256]{1,0:T(8,128)(2,1)S(1)}, u32[]{:S(2)}, u32[]{:S(2)}) collective-permute-start(bf16[128,256]{1,0:T(8,128)(2,1)} %get-tuple-element.50), channel_id=1, source_target_pairs={{0,2},{2,0},{4,6},{6,4},{1,3},{3,1},{5,7},{7,5},{8,10},{10,8},{12,... | collective-permute-start | bytes 196616 | tf_op jit(solution)/shard_map/ppermute | solution.py:212
  66.2 1.5 %collective-permute-start.21 = (bf16[128,256]{1,0:T(8,128)(2,1)}, bf16[128,256]{1,0:T(8,128)(2,1)S(1)}, u32[]{:S(2)}, u32[]{:S(2)}) collective-permute-start(bf16[128,256]{1,0:T(8,128)(2,1)} %get-tuple-element.52), channel_id=1, source_target_pairs={{0,6},{2,4},{4,2},{6,0},{1,7},{3,5},{5,3},{7,1},{8,14},{10,12},{12... | collective-permute-start | bytes 196616 | tf_op jit(solution)/shard_map/ppermute | solution.py:212
  67.7 6.1 %collective-permute-done.7.rb = bf16[2,144,512]{2,1,0:T(8,128)(2,1)S(1)} collective-permute-done((bf16[2,144,512]{2,1,0:T(8,128)(2,1)}, bf16[2,144,512]{2,1,0:T(8,128)(2,1)S(1)}, u32[]{:S(2)}, u32[]{:S(2)}) %collective-permute-start.7) | collective-permute-done | bytes 294944 | tf_op jit(solution)/shard_map/ppermute | solution.py:249
  74.5 2.1 %shard_map.66 = (bf16[128,256]{1,0:T(8,128)(2,1)}, bf16[128,256]{1,0:T(8,128)(2,1)}, bf16[128,256]{1,0:T(8,128)(2,1)}, bf16[128,256]{1,0:T(8,128)(2,1)}) custom-call(s32[2]{0:T(128)} %pad_add_fusion.where, f32[2,128,512]{2,1,0:T(8,128)} %get-tuple-element.33.own, f32[2,8,512]{2,1,0:T(8,128)} %get-tuple-element.34.lse, bf16[2,144,512]{2,1,0:T(8,128)(2,1)} %copy-done.8, ...), custom_call_target="tpu_custom_call" | custom-call | tf_op jit(solution)/shard_map/pallas_call | solution.py:251
  76.6 1.5 %collective-permute-start.10 = (bf16[128,256]{1,0:T(8,128)(2,1)}, bf16[128,256]{1,0:T(8,128)(2,1)S(1)}, u32[]{:S(2)}, u32[]{:S(2)}) collective-permute-start(bf16[128,256]{1,0:T(8,128)(2,1)} %get-tuple-element.40), channel_id=1, source_target_pairs={{0,6},{2,4},{4,2},{6,0},{1,7},{3,5},{5,3},{7,1},{8,14},{10,12},{12... | collective-permute-start | bytes 196616 | tf_op jit(solution)/shard_map/ppermute | solution.py:212
  78.6 1.5 %collective-permute-start.9 = (bf16[128,256]{1,0:T(8,128)(2,1)}, bf16[128,256]{1,0:T(8,128)(2,1)S(1)}, u32[]{:S(2)}, u32[]{:S(2)}) collective-permute-start(bf16[128,256]{1,0:T(8,128)(2,1)} %get-tuple-element.39), channel_id=1, source_target_pairs={{0,4},{2,6},{4,0},{6,2},{1,5},{3,7},{5,1},{7,3},{8,12},{10,14},{12... | collective-permute-start | bytes 196616 | tf_op jit(solution)/shard_map/ppermute | solution.py:212
  80.2 1.9 %collective-permute-done.10.refs_3_ = bf16[128,256]{1,0:T(8,128)(2,1)S(1)} collective-permute-done((bf16[128,256]{1,0:T(8,128)(2,1)}, bf16[128,256]{1,0:T(8,128)(2,1)S(1)}, u32[]{:S(2)}, u32[]{:S(2)}) %collective-permute-start.10) | collective-permute-done | bytes 65568 | tf_op jit(solution)/shard_map/ppermute | solution.py:212
  83.7 2.5 %shard_map.69 = bf16[128,2048]{1,0:T(8,128)(2,1)} custom-call(s32[2]{0:T(128)} %pad_add_fusion.where, s32[2]{0:T(128)} %slot.1, f32[2,64]{1,0:T(2,128)} %table.1, bf16[2,128,2048]{2,1,0:T(8,128)(2,1)} %past.1, bf16[128,256]{1,0:T(8,128)(2,1)} %get-tuple-element.37.refs_0_, bf16[128,256]{1,0:T(8,128)(2,1)} %copy-done.20, bf16[128,256]{1,0:T(8,128)(2,1)} %copy-done.21, ...), custom_call_target="tpu_custom_call" | custom-call | tf_op jit(solution)/shard_map/pallas_call | solution.py:259
  (95 shorter events, 16.9 us)
Async XLA Ops:
  3.3 8.9 %collective-permute-start.13 = (bf16[3,128,256]{2,1,0:T(8,128)(2,1)}, bf16[3,128,256]{2,1,0:T(8,128)(2,1)S(1)}, u32[]{:S(2)}, u32[]{:S(2)}) collective-permute-start(bf16[3,128,256]{2,1,0:T(8,128)(2,1)} %get-tuple-element.44), channel_id=1, source_target_pairs={{0,6},{2,4},{4,2},{6,0},{1,7},{3,5},{5,3},{7,1},{8,14},{10,12},{12... | collective-permute-start | bytes 589832 | tf_op jit(solution)/shard_map/ppermute | solution.py:212
  5.8 10.8 %collective-permute-start.12 = (bf16[3,128,256]{2,1,0:T(8,128)(2,1)}, bf16[3,128,256]{2,1,0:T(8,128)(2,1)S(1)}, u32[]{:S(2)}, u32[]{:S(2)}) collective-permute-start(bf16[3,128,256]{2,1,0:T(8,128)(2,1)} %get-tuple-element.43), channel_id=1, source_target_pairs={{0,4},{2,6},{4,0},{6,2},{1,5},{3,7},{5,1},{7,3},{8,12},{10,14},{12... | collective-permute-start | bytes 589832 | tf_op jit(solution)/shard_map/ppermute | solution.py:212
  6.3 10.3 %collective-permute-start.11 = (bf16[3,128,256]{2,1,0:T(8,128)(2,1)}, bf16[3,128,256]{2,1,0:T(8,128)(2,1)S(1)}, u32[]{:S(2)}, u32[]{:S(2)}) collective-permute-start(bf16[3,128,256]{2,1,0:T(8,128)(2,1)} %get-tuple-element.42), channel_id=1, source_target_pairs={{0,2},{2,0},{4,6},{6,4},{1,3},{3,1},{5,7},{7,5},{8,10},{10,8},{12,... | collective-permute-start | bytes 589832 | tf_op jit(solution)/shard_map/ppermute | solution.py:212
  6.8 18.4 %collective-permute-start.2 = (bf16[3,128,256]{2,1,0:T(8,128)(2,1)}, bf16[3,128,256]{2,1,0:T(8,128)(2,1)S(1)}, u32[]{:S(2)}, u32[]{:S(2)}) collective-permute-start(bf16[3,128,256]{2,1,0:T(8,128)(2,1)} %get-tuple-element.32), channel_id=1, source_target_pairs={{0,6},{2,4},{4,2},{6,0},{1,7},{3,5},{5,3},{7,1},{8,14},{10,12},{12... | collective-permute-start | bytes 589832 | tf_op jit(solution)/shard_map/ppermute | solution.py:212
  9.3 15.9 %collective-permute-start.1 = (bf16[3,128,256]{2,1,0:T(8,128)(2,1)}, bf16[3,128,256]{2,1,0:T(8,128)(2,1)S(1)}, u32[]{:S(2)}, u32[]{:S(2)}) collective-permute-start(bf16[3,128,256]{2,1,0:T(8,128)(2,1)} %get-tuple-element.31), channel_id=1, source_target_pairs={{0,4},{2,6},{4,0},{6,2},{1,5},{3,7},{5,1},{7,3},{8,12},{10,14},{12... | collective-permute-start | bytes 589832 | tf_op jit(solution)/shard_map/ppermute | solution.py:212
  12.5 11.4 %collective-permute-start = (bf16[3,128,256]{2,1,0:T(8,128)(2,1)S(1)}, bf16[3,128,256]{2,1,0:T(8,128)(2,1)S(1)}, u32[]{:S(2)}, u32[]{:S(2)}) collective-permute-start(bf16[3,128,256]{2,1,0:T(8,128)(2,1)S(1)} %copy-done.22), channel_id=1, source_target_pairs={{0,2},{2,0},{4,6},{6,4},{1,3},{3,1},{5,7},{7,5},{8,10},{10,8},{12,... | collective-permute-start | bytes 589832 | tf_op jit(solution)/shard_map/ppermute | solution.py:212
  16.6 10.8 %collective-permute-start.15 = (bf16[512,256]{1,0:T(8,128)(2,1)S(1)}, bf16[512,256]{1,0:T(8,128)(2,1)S(1)}, u32[]{:S(2)}, u32[]{:S(2)}) collective-permute-start(bf16[512,256]{1,0:T(8,128)(2,1)S(1)} %pad_maximum_fusion.3.q), channel_id=1, source_target_pairs={{16,8},{17,9},{18,10},{19,11},{20,12},{21,13},{22,14},{23,15}} | collective-permute-start | bytes 786440 | tf_op jit(solution)/shard_map/ppermute | solution.py:235
  17.3 18.5 %collective-permute-start.16 = (bf16[512,256]{1,0:T(8,128)(2,1)S(1)}, bf16[512,256]{1,0:T(8,128)(2,1)S(1)}, u32[]{:S(2)}, u32[]{:S(2)}) collective-permute-start(bf16[512,256]{1,0:T(8,128)(2,1)S(1)} %pad_maximum_fusion.3.q), channel_id=1, source_target_pairs={{24,8},{25,9},{26,10},{27,11},{28,12},{29,13},{30,14},{31,15}} | collective-permute-start | bytes 786440 | tf_op jit(solution)/shard_map/ppermute | solution.py:234
  23.9 16.7 %collective-permute-start.14 = (bf16[2,512,256]{2,1,0:T(8,128)(2,1)S(1)}, bf16[2,512,256]{2,1,0:T(8,128)(2,1)S(1)}, u32[]{:S(2)}, u32[]{:S(2)}) collective-permute-start(bf16[2,512,256]{2,1,0:T(8,128)(2,1)S(1)} %pad_maximum_fusion.1.kv), channel_id=1, source_target_pairs={{0,8},{16,24},{1,9},{17,25},{2,10},{18,26},{3,11},{19,27},{4,12},{... | collective-permute-start | bytes 1572872 | tf_op jit(solution)/shard_map/ppermute | solution.py:236
  25.3 20.4 %copy-start.1 = (bf16[2,512,256]{2,1,0:T(8,128)(2,1)}, bf16[2,512,256]{2,1,0:T(8,128)(2,1)S(1)}, u32[]{:S(2)}) copy-start(bf16[2,512,256]{2,1,0:T(8,128)(2,1)S(1)} %pad_maximum_fusion.kv) | copy-start | bytes 1572868
  25.3 24.5 %collective-permute-start.3 = (bf16[2,512,256]{2,1,0:T(8,128)(2,1)S(1)}, bf16[2,512,256]{2,1,0:T(8,128)(2,1)S(1)}, u32[]{:S(2)}, u32[]{:S(2)}) collective-permute-start(bf16[2,512,256]{2,1,0:T(8,128)(2,1)S(1)} %pad_maximum_fusion.kv), channel_id=1, source_target_pairs={{0,8},{16,24},{1,9},{17,25},{2,10},{18,26},{3,11},{19,27},{4,12},{... | collective-permute-start | bytes 1572872 | tf_op jit(solution)/shard_map/ppermute | solution.py:236
  26.7 19.0 %copy-start.3 = (bf16[512,256]{1,0:T(8,128)(2,1)}, bf16[512,256]{1,0:T(8,128)(2,1)S(1)}, u32[]{:S(2)}) copy-start(bf16[512,256]{1,0:T(8,128)(2,1)S(1)} %pad_maximum_fusion.2.q) | copy-start | bytes 786436
  26.7 21.0 %collective-permute-start.4 = (bf16[512,256]{1,0:T(8,128)(2,1)S(1)}, bf16[512,256]{1,0:T(8,128)(2,1)S(1)}, u32[]{:S(2)}, u32[]{:S(2)}) collective-permute-start(bf16[512,256]{1,0:T(8,128)(2,1)S(1)} %pad_maximum_fusion.2.q), channel_id=1, source_target_pairs={{16,8},{17,9},{18,10},{19,11},{20,12},{21,13},{22,14},{23,15}} | collective-permute-start | bytes 786440 | tf_op jit(solution)/shard_map/ppermute | solution.py:235
  27.4 20.3 %collective-permute-start.5 = (bf16[512,256]{1,0:T(8,128)(2,1)S(1)}, bf16[512,256]{1,0:T(8,128)(2,1)}, u32[]{:S(2)}, u32[]{:S(2)}) collective-permute-start(bf16[512,256]{1,0:T(8,128)(2,1)S(1)} %pad_maximum_fusion.2.q), channel_id=1, source_target_pairs={{24,8},{25,9},{26,10},{27,11},{28,12},{29,13},{30,14},{31,15}} | collective-permute-start | bytes 786440 | tf_op jit(solution)/shard_map/ppermute | solution.py:234
  45.7 11.2 %collective-permute-start.17 = (bf16[2,144,512]{2,1,0:T(8,128)(2,1)}, bf16[2,144,512]{2,1,0:T(8,128)(2,1)S(1)}, u32[]{:S(2)}, u32[]{:S(2)}) collective-permute-start(bf16[2,144,512]{2,1,0:T(8,128)(2,1)} %get-tuple-element.47), channel_id=1, source_target_pairs={{8,16},{9,17},{10,18},{11,19},{12,20},{13,21},{14,22},{15,23}} | collective-permute-start | bytes 884744 | tf_op jit(solution)/shard_map/ppermute | solution.py:250
  46.4 15.0 %collective-permute-start.18 = (bf16[2,144,512]{2,1,0:T(8,128)(2,1)}, bf16[2,144,512]{2,1,0:T(8,128)(2,1)S(1)}, u32[]{:S(2)}, u32[]{:S(2)}) collective-permute-start(bf16[2,144,512]{2,1,0:T(8,128)(2,1)} %get-tuple-element.48), channel_id=1, source_target_pairs={{8,24},{9,25},{10,26},{11,27},{12,28},{13,29},{14,30},{15,31}} | collective-permute-start | bytes 884744 | tf_op jit(solution)/shard_map/ppermute | solution.py:249
  54.9 12.8 %collective-permute-start.6 = (bf16[2,144,512]{2,1,0:T(8,128)(2,1)}, bf16[2,144,512]{2,1,0:T(8,128)(2,1)S(1)}, u32[]{:S(2)}, u32[]{:S(2)}) collective-permute-start(bf16[2,144,512]{2,1,0:T(8,128)(2,1)} %get-tuple-element.35), channel_id=1, source_target_pairs={{8,16},{9,17},{10,18},{11,19},{12,20},{13,21},{14,22},{15,23}} | collective-permute-start | bytes 884744 | tf_op jit(solution)/shard_map/ppermute | solution.py:250
  55.6 18.2 %collective-permute-start.7 = (bf16[2,144,512]{2,1,0:T(8,128)(2,1)}, bf16[2,144,512]{2,1,0:T(8,128)(2,1)S(1)}, u32[]{:S(2)}, u32[]{:S(2)}) collective-permute-start(bf16[2,144,512]{2,1,0:T(8,128)(2,1)} %get-tuple-element.36), channel_id=1, source_target_pairs={{8,24},{9,25},{10,26},{11,27},{12,28},{13,29},{14,30},{15,31}} | collective-permute-start | bytes 884744 | tf_op jit(solution)/shard_map/ppermute | solution.py:249
  64.2 14.5 %collective-permute-start.19 = (bf16[128,256]{1,0:T(8,128)(2,1)}, bf16[128,256]{1,0:T(8,128)(2,1)S(1)}, u32[]{:S(2)}, u32[]{:S(2)}) collective-permute-start(bf16[128,256]{1,0:T(8,128)(2,1)} %get-tuple-element.50), channel_id=1, source_target_pairs={{0,2},{2,0},{4,6},{6,4},{1,3},{3,1},{5,7},{7,5},{8,10},{10,8},{12,... | collective-permute-start | bytes 196616 | tf_op jit(solution)/shard_map/ppermute | solution.py:212
  65.8 14.4 %collective-permute-start.20 = (bf16[128,256]{1,0:T(8,128)(2,1)}, bf16[128,256]{1,0:T(8,128)(2,1)S(1)}, u32[]{:S(2)}, u32[]{:S(2)}) collective-permute-start(bf16[128,256]{1,0:T(8,128)(2,1)} %get-tuple-element.51), channel_id=1, source_target_pairs={{0,4},{2,6},{4,0},{6,2},{1,5},{3,7},{5,1},{7,3},{8,12},{10,14},{12... | collective-permute-start | bytes 196616 | tf_op jit(solution)/shard_map/ppermute | solution.py:212
  66.2 14.0 %collective-permute-start.21 = (bf16[128,256]{1,0:T(8,128)(2,1)}, bf16[128,256]{1,0:T(8,128)(2,1)S(1)}, u32[]{:S(2)}, u32[]{:S(2)}) collective-permute-start(bf16[128,256]{1,0:T(8,128)(2,1)} %get-tuple-element.52), channel_id=1, source_target_pairs={{0,6},{2,4},{4,2},{6,0},{1,7},{3,5},{5,3},{7,1},{8,14},{10,12},{12... | collective-permute-start | bytes 196616 | tf_op jit(solution)/shard_map/ppermute | solution.py:212
  76.6 5.4 %collective-permute-start.10 = (bf16[128,256]{1,0:T(8,128)(2,1)}, bf16[128,256]{1,0:T(8,128)(2,1)S(1)}, u32[]{:S(2)}, u32[]{:S(2)}) collective-permute-start(bf16[128,256]{1,0:T(8,128)(2,1)} %get-tuple-element.40), channel_id=1, source_target_pairs={{0,6},{2,4},{4,2},{6,0},{1,7},{3,5},{5,3},{7,1},{8,14},{10,12},{12... | collective-permute-start | bytes 196616 | tf_op jit(solution)/shard_map/ppermute | solution.py:212
  78.1 4.5 %collective-permute-start.8 = (bf16[128,256]{1,0:T(8,128)(2,1)}, bf16[128,256]{1,0:T(8,128)(2,1)S(1)}, u32[]{:S(2)}, u32[]{:S(2)}) collective-permute-start(bf16[128,256]{1,0:T(8,128)(2,1)} %get-tuple-element.38), channel_id=1, source_target_pairs={{0,2},{2,0},{4,6},{6,4},{1,3},{3,1},{5,7},{7,5},{8,10},{10,8},{12,... | collective-permute-start | bytes 196616 | tf_op jit(solution)/shard_map/ppermute | solution.py:212
  78.6 4.5 %collective-permute-start.9 = (bf16[128,256]{1,0:T(8,128)(2,1)}, bf16[128,256]{1,0:T(8,128)(2,1)S(1)}, u32[]{:S(2)}, u32[]{:S(2)}) collective-permute-start(bf16[128,256]{1,0:T(8,128)(2,1)} %get-tuple-element.39), channel_id=1, source_target_pairs={{0,4},{2,6},{4,0},{6,2},{1,5},{3,7},{5,1},{7,3},{8,12},{10,14},{12... | collective-permute-start | bytes 196616 | tf_op jit(solution)/shard_map/ppermute | solution.py:212
  (23 other events, 65.8 us)
